TPU v7x, 32 devices: a 4x2x2 block of a 4x4x8 slice. The times are simulated.
32 devices in a mesh: data: 4 (over y, z), ctx: 8 (over x, core).
Axes of the slice: x: 4, y: 2, z: 2, core: 2. Of those that a mesh axis runs over, the one named last changes fastest.
The devices are a block of a 4x4x8 slice.
Arguments:
- hidden: bfloat16 [1024, 5120], P(('data', 'ctx')), parts along dimension 0
- seq_lens: int32 [1024], P(('data', 'ctx')), parts along dimension 0
- w_query: bfloat16 [2, 5120, 4096], replicated
- w_key: bfloat16 [2, 5120, 1024], replicated
- w_value: bfloat16 [2, 5120, 1024], replicated
- w_out: bfloat16 [2, 4096, 5120], replicated
- k_prefix: bfloat16 [2, 8192, 8, 128], P(None, ('data', 'ctx')), parts along dimension 1
- v_prefix: bfloat16 [2, 8192, 8, 128], P(None, ('data', 'ctx')), parts along dimension 1
- k_suffix: bfloat16 [2, 1024, 32, 8, 128], P(None, ('data', 'ctx')), parts along dimension 1
- v_suffix: bfloat16 [2, 1024, 32, 8, 128], P(None, ('data', 'ctx')), parts along dimension 1
Outputs:
- output 1: bfloat16 [1024, 5120], P(('data', 'ctx')), parts along dimension 0
- output 2: bfloat16 [2, 1024, 32, 8, 128], P(None, ('data', 'ctx')), parts along dimension 1
- output 3: bfloat16 [2, 1024, 32, 8, 128], P(None, ('data', 'ctx')), parts along dimension 1
There are 4 independent parts. A program takes and returns all parts, laid end to end along the dimension named above; an argument that names none is the same for every part.
All inputs are finite; a program needn't handle non-finite values.
Results may differ from a plain program's by a relative error of at most 0.0105281.
Values are sent between devices in bfloat16 or wider.
A program may use at most 768 MiB of HBM per device.

v0:
```python
import functools

import jax
import jax.numpy as jnp
from jax import lax
from jax.experimental import pallas as pl
from jax.experimental.pallas import tpu as pltpu
from jax.sharding import PartitionSpec as P

MESH = pl.DeviceIdType.MESH
BF16 = jnp.bfloat16
F32 = jnp.float32
RING = 10
COLS = 512
LOG2E = 1.4426950408889634
FLOOR = float(jnp.finfo(jnp.float32).min)


def dot(a, b):
    return lax.dot_general(a, b, (((1,), (0,)), ((), ())), preferred_element_type=F32)


def dot_t(a, b):
    return lax.dot_general(a, b, (((1,), (1,)), ((), ())), preferred_element_type=F32)


def decode_kernel(ctx_size, hidden, lens, wq, wk, wv, wo, kpre, vpre, ksuf, vsuf, hid_out, kvn_out,
                  wq_ring, wkv_ring, w_sem, wo_buf, wo_sem, pst, pst_sem, pf32, psend, precv, ps_s, ps_r,
                  suf, suf_sem, xr, xr_sem, xh, fin_st, fin_rc, x_sem, acc_q, acc_kv, qkv_st, hq, hs_s, hs_r,
                  q_rc, q_s, q_r, qs, os, ls, sc, pb, o_st, lse_st, o_rc, lse_rc, o_s, o_r, l_s, l_r,
                  o_cat, oc_s, oc_r, acc_o):
    layers = wq.shape[0]
    dim = wq.shape[1]
    half = dim // 2
    kc = dim // 4
    rows, heads, hd = hidden.shape[0], kpre.shape[2], kpre.shape[3]
    group = wq.shape[2] // (heads * hd)
    span = kpre.shape[1]
    slots = ksuf.shape[2] // heads
    chips = ctx_size // 2
    order = (2, 1, 3, 0)
    scale = hd ** -0.5
    c2 = scale * LOG2E
    gq = group * hd
    nblk = half // COLS

    me = lax.axis_index("ctx")
    chip = me // 2
    core = me % 2
    other = 1 - core
    partner = chip * 2 + other
    pending = []

    def to(dev):
        return {"ctx": dev}

    def remote(src, dst, s_sem, r_sem, dev):
        return pltpu.make_async_remote_copy(src_ref=src, dst_ref=dst, send_sem=s_sem, recv_sem=r_sem,
                                            device_id=to(dev), device_id_type=MESH)

    def send(src, dst, s_sem, r_sem, dev):
        copy = remote(src, dst, s_sem, r_sem, dev)
        copy.start()
        pending.append(copy)

    def arrived(dst, r_sem, s_sem):
        remote(dst, dst, s_sem, r_sem, partner).wait_recv()

    def dest_chip(t):
        return (chip + order[t]) % chips

    def src_chip(t):
        return (chip + chips - order[t]) % chips

    def weight_copies(layer, t, hh, kk):
        slot = (layer * 16 + t * 4 + hh * 2 + kk) % RING
        g = dest_chip(t) * 2 + core
        row = pl.multiple_of(((core + hh) % 2) * half + kk * kc, 128)
        krows = pl.ds(row, kc)
        return (
            pltpu.make_async_copy(wq.at[layer, krows, pl.ds(pl.multiple_of(g * gq, gq), gq)],
                                  wq_ring.at[slot], w_sem.at[slot, 0]),
            pltpu.make_async_copy(wk.at[layer, krows, pl.ds(pl.multiple_of(g * hd, hd), hd)],
                                  wkv_ring.at[slot, :, 0:hd], w_sem.at[slot, 1]),
            pltpu.make_async_copy(wv.at[layer, krows, pl.ds(pl.multiple_of(g * hd, hd), hd)],
                                  wkv_ring.at[slot, :, hd:2 * hd], w_sem.at[slot, 2]),
        )

    def fetch_weights(layer, first, last):
        for n in range(first, min(last, 4 * chips)):
            for copy in weight_copies(layer, n // 4, (n // 2) % 2, n % 2):
                copy.start()

    def wo_copy(layer, tc, nb):
        return pltpu.make_async_copy(
            wo.at[layer, pl.ds(pl.multiple_of(tc * 2 * gq, 2 * gq), 2 * gq),
                  pl.ds(pl.multiple_of(core * half + nb * COLS, COLS), COLS)],
            wo_buf.at[tc, nb], wo_sem.at[tc, nb])

    def fetch_wo(layer, tc):
        for nb in range(nblk):
            wo_copy(layer, tc, nb).start()

    def prefix_copies(layer):
        return (pltpu.make_async_copy(kpre.at[layer], pst.at[0], pst_sem.at[0]),
                pltpu.make_async_copy(vpre.at[layer], pst.at[1], pst_sem.at[1]))

    def suffix_copies(layer):
        return (pltpu.make_async_copy(ksuf.at[layer], suf.at[0], suf_sem.at[0]),
                pltpu.make_async_copy(vsuf.at[layer], suf.at[1], suf_sem.at[1]))

    def relayout_prefix(layer):
        for copy in prefix_copies(layer):
            copy.wait()
        step = 64

        @pl.loop(0, 2)
        def _(kv):
            @pl.loop(0, span // step)
            def _(blk):
                base = pl.multiple_of(blk * step, step)
                pf32[...] = pst[kv, pl.ds(base, step)].astype(F32).reshape(step * heads, hd)
                for g in range(heads):
                    psend[layer, g, kv, pl.ds(base, step), :] = pf32[pl.ds(g, step, stride=heads), :].astype(BF16)

    def send_prefix(layer):
        for d in (4, 5, 3, 2, 6, 7, 1):
            dev = (me + d) % ctx_size
            send(psend.at[layer, dev], precv.at[layer, :, me], ps_s.at[layer, dev], ps_r.at[layer, me], dev)
        for kv in range(2):
            precv[layer, kv, me] = psend[layer, me, kv]

    def await_prefix(layer):
        for d in (1, 7, 2, 6, 3, 5, 4):
            src = (me + d) % ctx_size
            arrived(precv.at[layer, :, src], ps_r.at[layer, src], ps_s.at[layer, src])

    def project(layer, t):
        acc_q[...] = jnp.zeros_like(acc_q)
        acc_kv[...] = jnp.zeros_like(acc_kv)

        for n in range(4 * t, 4 * t + 4):
            hh, kk = (n // 2) % 2, n % 2
            slot = (layer * 16 + n) % RING
            for copy in weight_copies(layer, t, hh, kk):
                copy.wait()
            lhs = xh[layer, (core + hh) % 2, :, kk * kc:(kk + 1) * kc]
            acc_q[...] += dot(lhs, wq_ring[slot])
            acc_kv[...] += dot(lhs, wkv_ring[slot])
            fetch_weights(layer, n + RING, n + RING + 1)
            if layer == 0 and t == 2:
                fetch_wo(0, n % 4)

        q = acc_q[...].astype(BF16)
        kv = acc_kv[...].astype(BF16)
        for cr in range(2):
            part = slice(cr * rows, (cr + 1) * rows)
            for j in range(group):
                qkv_st[layer, t, cr, j] = q[part, j * hd:(j + 1) * hd]
            qkv_st[layer, t, cr, group] = kv[part, 0:hd]
            qkv_st[layer, t, cr, group + 1] = kv[part, hd:2 * hd]
        tc = dest_chip(t)
        if order[t] != 0:
            send(qkv_st.at[layer, t, :, 0:group], q_rc.at[layer, chip], q_s.at[layer, t], q_r.at[layer, chip],
                 tc * 2 + core)
        else:
            q_rc[layer, chip] = qkv_st[layer, t, :, 0:group]
        g = tc * 2 + core
        send(qkv_st.at[layer, t, other], hq.at[layer, g], hs_s.at[layer, t], hs_r.at[layer, t], partner)
        hq[layer, g] = qkv_st[layer, t, core]

    def suffix_attention(layer):
        for t in range(chips):
            arrived(hq.at[layer, dest_chip(t) * 2 + other], hs_r.at[layer, t], hs_s.at[layer, t])
        for g in range(heads):
            for j in range(group):
                qs[pl.ds(g * group + j, rows, stride=heads * group), :] = hq[layer, g, j].astype(F32)
        for copy in suffix_copies(layer):
            copy.wait()
        qh = heads * group
        row_id = lax.broadcasted_iota(jnp.int32, (qh, slots * heads), 0)
        col_id = lax.broadcasted_iota(jnp.int32, (qh, slots * heads), 1)
        slot_of = jnp.where((row_id // group) == (col_id % heads), col_id // heads, slots)
        step = 8

        @pl.loop(0, rows // step)
        def _(blk):
            for i in range(step):
                b = blk * step + i
                base = pl.multiple_of(b * qh, qh)
                s = dot_t(qs[pl.ds(base, qh), :].astype(BF16), suf[0, b])
                s = jnp.where(slot_of < lens[b], s, FLOOR)
                m = jnp.max(s, axis=1, keepdims=True)
                e = jnp.exp2((s - m) * c2)
                mass = jnp.sum(e, axis=1, keepdims=True)
                val = dot(e.astype(BF16), suf[1, b])
                os[pl.ds(base, qh), :] = val * (1.0 / mass)
                ls[pl.ds(base, qh), :] = jnp.broadcast_to(m * scale + jnp.log(mass), (qh, hd))

    def prefix_attention(layer, t):
        src = src_chip(t)
        if order[t] != 0:
            arrived(q_rc.at[layer, src], q_r.at[layer, src], q_s.at[layer, t])
        q = q_rc[layer, src].reshape(2 * group * rows, hd)
        peak = None
        for s in range(ctx_size):
            part = dot_t(q, precv[layer, 0, s])
            sc[s] = part
            for lo in range(0, span, 128):
                piece = part[:, lo:lo + 128]
                peak = piece if peak is None else jnp.maximum(peak, piece)
        m = jnp.max(peak, axis=1, keepdims=True)
        mass = jnp.zeros((2 * group * rows, 128), F32)
        for s in range(ctx_size):
            e = jnp.exp2((sc[s] - m) * c2)
            for lo in range(0, span, 128):
                mass = mass + e[:, lo:lo + 128]
            pb[:, s * span:(s + 1) * span] = e.astype(BF16)
        mass = jnp.sum(mass, axis=1, keepdims=True)
        vals = dot(pb[...], precv[layer, 1].reshape(ctx_size * span, hd))
        out = (vals * (1.0 / mass)).astype(BF16)
        lse = jnp.broadcast_to(m * scale + jnp.log(mass), (2 * group * rows, 128)).T
        for cr in range(2):
            part = group * rows
            o_st[layer, t, cr] = out[cr * part:(cr + 1) * part].reshape(group, rows, hd)
            lse_st[layer, t, cr] = lse[0:8, cr * part:(cr + 1) * part]
        if order[t] != 0:
            for cr in range(2):
                dev = src * 2 + cr
                send(lse_st.at[layer, t, cr], lse_rc.at[layer, me], l_s.at[layer, t, cr], l_r.at[layer, me], dev)
                send(o_st.at[layer, t, cr], o_rc.at[layer, me], o_s.at[layer, t, cr], o_r.at[layer, me], dev)
        else:
            send(lse_st.at[layer, t, other], lse_rc.at[layer, me], l_s.at[layer, t, 0], l_r.at[layer, me], partner)
            send(o_st.at[layer, t, other], o_rc.at[layer, me], o_s.at[layer, t, 0], o_r.at[layer, me], partner)
            lse_rc[layer, me] = lse_st[layer, t, core]
            o_rc[layer, me] = o_st[layer, t, core]

    def combine(layer, t):
        tc = dest_chip(t)
        for par in range(2):
            if order[t] != 0:
                g = tc * 2 + par
                arrived(lse_rc.at[layer, g], l_r.at[layer, g], l_s.at[layer, t, 0])
                arrived(o_rc.at[layer, g], o_r.at[layer, g], o_s.at[layer, t, 0])
            elif par == 0:
                arrived(lse_rc.at[layer, partner], l_r.at[layer, partner], l_s.at[layer, t, 0])
                arrived(o_rc.at[layer, partner], o_r.at[layer, partner], o_s.at[layer, t, 0])
        for par in range(2):
            g = tc * 2 + par
            lse_p = jnp.broadcast_to(lse_rc[layer, g, 0:1, :], (group * rows, 128)).T
            k_new = hq[layer, g, group].astype(F32)
            v_new = hq[layer, g, group + 1].astype(F32)
            for j in range(group):
                h = g * group + j
                picked = pl.ds(h, rows, stride=heads * group)
                lp = lse_p[j * rows:(j + 1) * rows]
                lo = ls[picked, :]
                sn = jnp.sum(hq[layer, g, j].astype(F32) * k_new, axis=1, keepdims=True) * scale
                top = jnp.maximum(jnp.maximum(lp, lo), sn)
                wp = jnp.exp(lp - top)
                wo_ = jnp.exp(lo - top)
                wn = jnp.exp(sn - top)
                mixed = wp * o_rc[layer, g, j].astype(F32) + wo_ * os[picked, :] + wn * v_new
                at = (par * group + j) * hd
                o_cat[layer, core, tc, :, at:at + hd] = (mixed / (wp + wo_ + wn)).astype(BF16)
        send(o_cat.at[layer, core, tc], o_cat.at[layer, core, tc], oc_s.at[layer, t], oc_r.at[layer, t], partner)

    def project_out(layer, t):
        tc = dest_chip(t)
        arrived(o_cat.at[layer, other, tc], oc_r.at[layer, t], oc_s.at[layer, t])
        lhs = jnp.concatenate([o_cat[layer, 0, tc], o_cat[layer, 1, tc]], axis=0)

        @pl.loop(0, nblk)
        def _(nb):
            wo_copy(layer, tc, nb).wait()
            upd = dot(lhs, wo_buf[tc, nb])
            if t == 0:
                acc_o[nb] = upd
            else:
                acc_o[nb] += upd
            if layer + 1 < layers:
                wo_copy(layer + 1, tc, nb).start()

    for copy in prefix_copies(0):
        copy.start()
    fetch_weights(0, 0, 4)
    barrier = pltpu.get_barrier_semaphore()
    for d in range(1, ctx_size):
        pl.semaphore_signal(barrier, inc=1, device_id=to((me + d) % ctx_size), device_id_type=MESH)
    pl.semaphore_wait(barrier, ctx_size - 1)
    send(hidden, xr.at[core], xr_sem.at[0], xr_sem.at[1], partner)
    fetch_weights(0, 4, RING)
    xr[core] = hidden[...]
    relayout_prefix(0)
    send_prefix(0)
    arrived(xr.at[other], xr_sem.at[1], xr_sem.at[0])
    for sd in range(2):
        for cr in range(2):
            xh[0, sd, cr * rows:(cr + 1) * rows, :] = xr[cr, :, sd * half:(sd + 1) * half]

    for layer in range(layers):
        for t in range(chips):
            project(layer, t)
            if layer == 0 and t == 1:
                for copy in suffix_copies(0):
                    copy.start()
        if layer + 1 < layers:
            for copy in prefix_copies(layer + 1):
                copy.start()
            fetch_weights(layer + 1, 0, RING)
            suffix_attention(layer)
            for copy in suffix_copies(layer + 1):
                copy.start()
            relayout_prefix(layer + 1)
        await_prefix(layer)
        for t in range(chips):
            prefix_attention(layer, t)
        if layer + 1 < layers:
            send_prefix(layer + 1)
        else:
            suffix_attention(layer)
        for t in range(chips):
            combine(layer, t)
            if t > 0:
                project_out(layer, t - 1)
        project_out(layer, chips - 1)
        for nb in range(nblk):
            cols = slice(nb * COLS, (nb + 1) * COLS)
            new = (xh[layer, core, :, cols].astype(F32) + acc_o[nb].astype(BF16).astype(F32)).astype(BF16)
            if layer + 1 < layers:
                xh[layer + 1, core, :, cols] = new
            else:
                for cr in range(2):
                    fin_st[cr, :, cols] = new[cr * rows:(cr + 1) * rows]
        if layer + 1 < layers:
            send(xh.at[layer + 1, core], xh.at[layer + 1, core], x_sem.at[0, 0], x_sem.at[0, 1], partner)
            arrived(xh.at[layer + 1, other], x_sem.at[0, 1], x_sem.at[0, 0])
    send(fin_st.at[other], fin_rc, x_sem.at[1, 0], x_sem.at[1, 1], partner)
    hid_out[core] = fin_st[core]
    for layer in range(layers):
        for g in range(heads):
            for i in range(2):
                kvn_out[layer, g, i] = hq[layer, g, group + i]
    arrived(fin_rc, x_sem.at[1, 1], x_sem.at[1, 0])
    hid_out[other] = fin_rc[...]
    for copy in pending:
        copy.wait_send()


def cache_kernel(lens, hid, kvn, ksuf, vsuf, hid_out, kout, vout, buf, tiles, in_sem, out_sem):
    layers, batch = ksuf.shape[0], ksuf.shape[1]
    heads, hd = ksuf.shape[3], ksuf.shape[4]
    half = hid.shape[2]
    step = 8
    parts = batch // step
    srcs, dsts = (ksuf, vsuf), (kout, vout)

    def copies(layer, i, part, out):
        here = pl.ds(part * step, step)
        at = (layer * 2 + i) * parts + part
        if out:
            return pltpu.make_async_copy(buf.at[layer, i, here], dsts[i].at[layer, here], out_sem.at[at])
        return pltpu.make_async_copy(srcs[i].at[layer, here], buf.at[layer, i, here], in_sem.at[at])

    todo = [(layer, i, part) for layer in range(layers) for i in range(2) for part in range(parts)]
    for layer, i, part in todo:
        copies(layer, i, part, False).start()
    for sd in range(2):
        hid_out[:, sd * half:(sd + 1) * half] = hid[sd]
    for layer in range(layers):
        for i in range(2):
            for g in range(heads):
                tiles[layer, i, pl.ds(g, batch, stride=heads), :] = kvn[layer, g, i].astype(F32)
    for layer, i, part in todo:
        copies(layer, i, part, False).wait()
        for b in range(part * step, (part + 1) * step):
            buf[layer, i, b, lens[b]] = tiles[layer, i, b * heads:(b + 1) * heads, :].astype(BF16)
        copies(layer, i, part, True).start()
    for layer, i, part in todo:
        copies(layer, i, part, True).wait()


def solution(mesh):
    ctx_size = mesh.shape["ctx"]
    home = ("data", "ctx")
    row_spec, lens_spec, whole = P(home, None), P(home), P()
    prefix_spec = P(None, home, None, None)
    cache_spec = P(None, home, None, None, None)

    def local_step(hidden, seq_lens, w_query, w_key, w_value, w_out, k_prefix, v_prefix, k_suffix, v_suffix):
        layers, dim, q_width = w_query.shape
        rows = hidden.shape[0]
        span, heads, hd = k_prefix.shape[1:]
        slots = k_suffix.shape[2]
        group = q_width // (heads * hd)
        chips = ctx_size // 2
        half, kc = dim // 2, dim // 4
        nblk = half // COLS
        qh = heads * group
        vmem, smem, anym = pltpu.VMEM, pltpu.SMEM, pl.ANY
        dma = pltpu.SemaphoreType.DMA
        spec = pl.BlockSpec
        scratch = [
            vmem((RING, kc, group * hd), BF16), vmem((RING, kc, 2 * hd), BF16), dma((RING, 3)),
            vmem((chips, nblk, 2 * group * hd, COLS), BF16), dma((chips, nblk)),
            vmem((2, span, heads, hd), BF16), dma((2,)), vmem((64 * heads, hd), F32),
            vmem((layers, ctx_size, 2, span, hd), BF16), vmem((layers, 2, ctx_size, span, hd), BF16),
            dma((layers, ctx_size)), dma((layers, ctx_size)),
            vmem((2, rows, slots * heads, hd), BF16), dma((2,)),
            vmem((2, rows, dim), BF16), dma((2,)),
            vmem((layers, 2, 2 * rows, half), BF16), vmem((2, rows, half), BF16), vmem((rows, half), BF16), dma((2, 2)),
            vmem((2 * rows, group * hd), F32), vmem((2 * rows, 2 * hd), F32),
            vmem((layers, chips, 2, group + 2, rows, hd), BF16), vmem((layers, heads, group + 2, rows, hd), BF16),
            dma((layers, chips)), dma((layers, chips)),
            vmem((layers, chips, 2, group, rows, hd), BF16), dma((layers, chips)), dma((layers, chips)),
            vmem((rows * qh, hd), F32), vmem((rows * qh, hd), F32), vmem((rows * qh, hd), F32),
            vmem((ctx_size, 2 * group * rows, span), F32), vmem((2 * group * rows, ctx_size * span), BF16),
            vmem((layers, chips, 2, group, rows, hd), BF16), vmem((layers, chips, 2, 8, 128), F32),
            vmem((layers, heads, group, rows, hd), BF16), vmem((layers, heads, 8, 128), F32),
            dma((layers, chips, 2)), dma((layers, heads)), dma((layers, chips, 2)), dma((layers, heads)),
            vmem((layers, 2, chips, rows, 2 * group * hd), BF16), dma((layers, chips)), dma((layers, chips)),
            vmem((nblk, 2 * rows, COLS), F32),
        ]
        hid, kvn = pl.pallas_call(
            functools.partial(decode_kernel, ctx_size),
            name="decode",
            out_shape=(jax.ShapeDtypeStruct((2, rows, half), BF16),
                       jax.ShapeDtypeStruct((layers, heads, 2, rows, hd), BF16)),
            in_specs=[spec(memory_space=vmem), spec(memory_space=smem)] + [spec(memory_space=anym)] * 8,
            out_specs=(spec(memory_space=vmem), spec(memory_space=vmem)),
            scratch_shapes=scratch,
            compiler_params=pltpu.CompilerParams(collective_id=0, has_side_effects=True, vmem_limit_bytes=67043328),
        )(hidden, seq_lens, w_query, w_key, w_value, w_out, k_prefix, v_prefix,
          k_suffix.reshape(layers, rows, slots * heads, hd), v_suffix.reshape(layers, rows, slots * heads, hd))
        copies = layers * 2 * (rows // 8)
        return pl.pallas_call(
            cache_kernel,
            name="caches",
            out_shape=(jax.ShapeDtypeStruct(hidden.shape, BF16), jax.ShapeDtypeStruct(k_suffix.shape, BF16),
                       jax.ShapeDtypeStruct(v_suffix.shape, BF16)),
            in_specs=[spec(memory_space=smem), spec(memory_space=vmem), spec(memory_space=vmem),
                      spec(memory_space=anym), spec(memory_space=anym)],
            out_specs=(spec(memory_space=vmem), spec(memory_space=anym), spec(memory_space=anym)),
            scratch_shapes=[vmem((layers, 2, rows, slots, heads, hd), BF16), vmem((layers, 2, rows * heads, hd), F32),
                            dma((copies,)), dma((copies,))],
            compiler_params=pltpu.CompilerParams(vmem_limit_bytes=67043328),
        )(seq_lens, hid, kvn, k_suffix, v_suffix)

    return jax.shard_map(local_step, mesh=mesh,
                         in_specs=(row_spec, lens_spec, whole, whole, whole, whole, prefix_spec, prefix_spec, cache_spec, cache_spec),
                         out_specs=(row_spec, cache_spec, cache_spec), check_vma=False)
```

profile of v0, /device:TPU:81, one launch (start us, length us, event | category | flops | bytes accessed | tf_op | source)
XLA Modules:
  0.0 91.7 jit_solution(12244773694333529453)
XLA Ops:
  0.6 82.5 %decode.1 = (bf16[2,32,2560]{2,1,0:T(8,128)(2,1)}, bf16[2,8,2,32,128]{4,3,2,1,0:T(8,128)(2,1)}) custom-call(bf16[32,5120]{1,0:T(8,128)(2,1)} %hidden.1, s32[32]{0:T(128)} %lens.3, bf16[2,5120,4096]{2,1,0:T(8,128)(2,1)} %wq.1, bf16[2,5120,1024]{2,1,0:T(8,128)(2,1)} %wk.1, bf16[2,5120,1024]{2,1,0:T(8,128)(2,1)} %wv.1, bf16[2,4096,5120]{2,1,0:T(8,128)(2,1)} %wo.1, ...), custom_call_target="tpu_custom_call" | custom-call | tf_op jit(solution)/shard_map/decode/pallas_call | solution.py:424
  83.2 8.3 %caches.1 = (bf16[32,5120]{1,0:T(8,128)(2,1)}, bf16[2,32,32,8,128]{4,3,2,1,0:T(8,128)(2,1)}, bf16[2,32,32,8,128]{4,3,2,1,0:T(8,128)(2,1)}) custom-call(s32[32]{0:T(128)} %lens.3, bf16[2,32,2560]{2,1,0:T(8,128)(2,1)} %get-tuple-element.5.hid, bf16[2,8,2,32,128]{4,3,2,1,0:T(8,128)(2,1)} %get-tuple-element.6.kvn, bf16[2,32,32,8,128]{4,3,2,1,0:T(8,128)(2,1)} %ksuf.1, ...), custom_call_target="tpu_custom_call" | custom-call | tf_op jit(solution)/shard_map/caches/pallas_call | solution.py:436
where the time goes:
time: 91.8 us; the launch traced here: 91.7 us
  Pallas kernels  90.9 us (99%)
    pallas_call x1, Pallas kernels, local_step(): pl.pallas_call(functools.partial(decode_kernel, ctx_size), name='decode',...  82.5 us
    pallas_call x1, Pallas kernels, local_step(): pl.pallas_call(cache_kernel, name='caches', out_shape=(jax.ShapeDtypeStru...  8.33 us

commit v1 on v0

--- a/solution.py
+++ b/solution.py
@@ -24,16 +24,17 @@
     return lax.dot_general(a, b, (((1,), (1,)), ((), ())), preferred_element_type=F32)
 
 
-def decode_kernel(ctx_size, hidden, lens, wq, wk, wv, wo, kpre, vpre, ksuf, vsuf, hid_out, kvn_out,
-                  wq_ring, wkv_ring, w_sem, wo_buf, wo_sem, pst, pst_sem, pf32, psend, precv, ps_s, ps_r,
-                  suf, suf_sem, xr, xr_sem, xh, fin_st, fin_rc, x_sem, acc_q, acc_kv, qkv_st, hq, hs_s, hs_r,
-                  q_rc, q_s, q_r, qs, os, ls, sc, pb, o_st, lse_st, o_rc, lse_rc, o_s, o_r, l_s, l_r,
+def decode_kernel(ctx_size, hidden, lens_hbm, wq, wk, wv, wo, kpre, vpre, ksuf, vsuf, hid_out, kvn_out,
+                  lens, io_sem, ring, w_sem, wo_buf, wo_sem, pst, pst_sem, pf32, psend, precv, ps_s, ps_r,
+                  suf, suf_sem, xh, fin_st, fin_rc, x_sem, acc, qkv_st, hq, hs_s, hs_r,
+                  q_rc, q_s, q_r, qs, os, ls, lm, sc, pb, o_st, lse_st, o_rc, lse_rc, o_s, o_r, l_s, l_r,
                   o_cat, oc_s, oc_r, acc_o):
     layers = wq.shape[0]
     dim = wq.shape[1]
     half = dim // 2
     kc = dim // 4
     rows, heads, hd = hidden.shape[0], kpre.shape[2], kpre.shape[3]
+    qh = (wq.shape[2] // hd)
     group = wq.shape[2] // (heads * hd)
     span = kpre.shape[1]
     slots = ksuf.shape[2] // heads
@@ -72,23 +73,27 @@
     def src_chip(t):
         return (chip + chips - order[t]) % chips
 
-    def weight_copies(layer, t, hh, kk):
-        slot = (layer * 16 + t * 4 + hh * 2 + kk) % RING
+    def weight_place(layer, n):
+        if layer == 0:
+            return n // 4, (n // 2) % 2, n % 2
+        return (n // 2) % chips, n // (2 * chips), n % 2
+
+    def weight_copies(layer, n):
+        t, hh, kk = weight_place(layer, n)
+        slot = (layer * 4 * chips + n) % RING
         g = dest_chip(t) * 2 + core
-        row = pl.multiple_of(((core + hh) % 2) * half + kk * kc, 128)
-        krows = pl.ds(row, kc)
+        krows = pl.ds(pl.multiple_of(((core + hh) % 2) * half + kk * kc, 128), kc)
+        qcols = pl.ds(pl.multiple_of(g * gq, gq), gq)
+        kcols = pl.ds(pl.multiple_of(g * hd, hd), hd)
         return (
-            pltpu.make_async_copy(wq.at[layer, krows, pl.ds(pl.multiple_of(g * gq, gq), gq)],
-                                  wq_ring.at[slot], w_sem.at[slot, 0]),
-            pltpu.make_async_copy(wk.at[layer, krows, pl.ds(pl.multiple_of(g * hd, hd), hd)],
-                                  wkv_ring.at[slot, :, 0:hd], w_sem.at[slot, 1]),
-            pltpu.make_async_copy(wv.at[layer, krows, pl.ds(pl.multiple_of(g * hd, hd), hd)],
-                                  wkv_ring.at[slot, :, hd:2 * hd], w_sem.at[slot, 2]),
+            pltpu.make_async_copy(wq.at[layer, krows, qcols], ring.at[slot, :, 0:gq], w_sem.at[slot, 0]),
+            pltpu.make_async_copy(wk.at[layer, krows, kcols], ring.at[slot, :, gq:gq + hd], w_sem.at[slot, 1]),
+            pltpu.make_async_copy(wv.at[layer, krows, kcols], ring.at[slot, :, gq + hd:gq + 2 * hd], w_sem.at[slot, 2]),
         )
 
     def fetch_weights(layer, first, last):
         for n in range(first, min(last, 4 * chips)):
-            for copy in weight_copies(layer, n // 4, (n // 2) % 2, n % 2):
+            for copy in weight_copies(layer, n):
                 copy.start()
 
     def wo_copy(layer, tc, nb):
@@ -109,56 +114,61 @@
         return (pltpu.make_async_copy(ksuf.at[layer], suf.at[0], suf_sem.at[0]),
                 pltpu.make_async_copy(vsuf.at[layer], suf.at[1], suf_sem.at[1]))
 
-    def relayout_prefix(layer):
-        for copy in prefix_copies(layer):
-            copy.wait()
+    def relayout_prefix(layer, kv):
+        prefix_copies(layer)[kv].wait()
         step = 64
 
-        @pl.loop(0, 2)
-        def _(kv):
-            @pl.loop(0, span // step)
-            def _(blk):
-                base = pl.multiple_of(blk * step, step)
-                pf32[...] = pst[kv, pl.ds(base, step)].astype(F32).reshape(step * heads, hd)
-                for g in range(heads):
-                    psend[layer, g, kv, pl.ds(base, step), :] = pf32[pl.ds(g, step, stride=heads), :].astype(BF16)
-
-    def send_prefix(layer):
+        @pl.loop(0, span // step)
+        def _(blk):
+            base = pl.multiple_of(blk * step, step)
+            pf32[...] = pst[kv, pl.ds(base, step)].astype(F32).reshape(step * heads, hd)
+            for g in range(heads):
+                psend[layer, g, kv, pl.ds(base, step), :] = pf32[pl.ds(g, step, stride=heads), :].astype(BF16)
+
+    def send_prefix(layer, kv):
         for d in (4, 5, 3, 2, 6, 7, 1):
             dev = (me + d) % ctx_size
-            send(psend.at[layer, dev], precv.at[layer, :, me], ps_s.at[layer, dev], ps_r.at[layer, me], dev)
-        for kv in range(2):
-            precv[layer, kv, me] = psend[layer, me, kv]
+            send(psend.at[layer, dev, kv], precv.at[layer, kv, me], ps_s.at[layer, kv, dev], ps_r.at[layer, kv, me], dev)
+        precv[layer, kv, me] = psend[layer, me, kv]
 
     def await_prefix(layer):
         for d in (1, 7, 2, 6, 3, 5, 4):
             src = (me + d) % ctx_size
-            arrived(precv.at[layer, :, src], ps_r.at[layer, src], ps_s.at[layer, src])
+            for kv in range(2):
+                arrived(precv.at[layer, kv, src], ps_r.at[layer, kv, src], ps_s.at[layer, kv, src])
+
+    def dots(layer, chunks):
+        for n in chunks:
+            for copy in weight_copies(layer, n):
+                copy.wait()
+        total = None
+        for n in chunks:
+            _, hh, kk = weight_place(layer, n)
+            slot = (layer * 4 * chips + n) % RING
+            part = dot(xh[layer, (core + hh) % 2, :, kk * kc:(kk + 1) * kc], ring[slot])
+            total = part if total is None else total + part
+        return total
 
     def project(layer, t):
-        acc_q[...] = jnp.zeros_like(acc_q)
-        acc_kv[...] = jnp.zeros_like(acc_kv)
-
-        for n in range(4 * t, 4 * t + 4):
-            hh, kk = (n // 2) % 2, n % 2
-            slot = (layer * 16 + n) % RING
-            for copy in weight_copies(layer, t, hh, kk):
-                copy.wait()
-            lhs = xh[layer, (core + hh) % 2, :, kk * kc:(kk + 1) * kc]
-            acc_q[...] += dot(lhs, wq_ring[slot])
-            acc_kv[...] += dot(lhs, wkv_ring[slot])
+        if layer == 0:
+            chunks = range(4 * t, 4 * t + 4)
+            total = dots(layer, chunks)
+        else:
+            chunks = range(2 * chips + 2 * t, 2 * chips + 2 * t + 2)
+            total = acc[t] + dots(layer, chunks)
+        qkv = total.astype(BF16)
+        for n in chunks:
             fetch_weights(layer, n + RING, n + RING + 1)
-            if layer == 0 and t == 2:
-                fetch_wo(0, n % 4)
-
-        q = acc_q[...].astype(BF16)
-        kv = acc_kv[...].astype(BF16)
+        if layer == 0 and t >= 2:
+            fetch_wo(0, 2 * (t - 2))
+            fetch_wo(0, 2 * (t - 2) + 1)
+
         for cr in range(2):
             part = slice(cr * rows, (cr + 1) * rows)
             for j in range(group):
-                qkv_st[layer, t, cr, j] = q[part, j * hd:(j + 1) * hd]
-            qkv_st[layer, t, cr, group] = kv[part, 0:hd]
-            qkv_st[layer, t, cr, group + 1] = kv[part, hd:2 * hd]
+                qkv_st[layer, t, cr, j] = qkv[part, j * hd:(j + 1) * hd]
+            for i in range(2):
+                qkv_st[layer, t, cr, group + i] = qkv[part, gq + i * hd:gq + (i + 1) * hd]
         tc = dest_chip(t)
         if order[t] != 0:
             send(qkv_st.at[layer, t, :, 0:group], q_rc.at[layer, chip], q_s.at[layer, t], q_r.at[layer, chip],
@@ -177,7 +187,6 @@
                 qs[pl.ds(g * group + j, rows, stride=heads * group), :] = hq[layer, g, j].astype(F32)
         for copy in suffix_copies(layer):
             copy.wait()
-        qh = heads * group
         row_id = lax.broadcasted_iota(jnp.int32, (qh, slots * heads), 0)
         col_id = lax.broadcasted_iota(jnp.int32, (qh, slots * heads), 1)
         slot_of = jnp.where((row_id // group) == (col_id % heads), col_id // heads, slots)
@@ -196,6 +205,21 @@
                 val = dot(e.astype(BF16), suf[1, b])
                 os[pl.ds(base, qh), :] = val * (1.0 / mass)
                 ls[pl.ds(base, qh), :] = jnp.broadcast_to(m * scale + jnp.log(mass), (qh, hd))
+
+        for g in range(heads):
+            k_new = hq[layer, g, group].astype(F32)
+            v_new = hq[layer, g, group + 1].astype(F32)
+            for j in range(group):
+                h = g * group + j
+                picked = pl.ds(h, rows, stride=qh)
+                lo = ls[picked, :]
+                sn = jnp.sum(hq[layer, g, j].astype(F32) * k_new, axis=1, keepdims=True) * scale
+                top = jnp.maximum(lo, sn)
+                w_old = jnp.exp(lo - top)
+                w_new = jnp.exp(sn - top)
+                mass = w_old + w_new
+                qs[h * rows:(h + 1) * rows, :] = (w_old * os[picked, :] + w_new * v_new) / mass
+                lm[h * rows:(h + 1) * rows, :] = top + jnp.log(mass)
 
     def prefix_attention(layer, t):
         src = src_chip(t)
@@ -248,21 +272,16 @@
         for par in range(2):
             g = tc * 2 + par
             lse_p = jnp.broadcast_to(lse_rc[layer, g, 0:1, :], (group * rows, 128)).T
-            k_new = hq[layer, g, group].astype(F32)
-            v_new = hq[layer, g, group + 1].astype(F32)
             for j in range(group):
-                h = g * group + j
-                picked = pl.ds(h, rows, stride=heads * group)
+                here = pl.ds(pl.multiple_of((g * group + j) * rows, rows), rows)
                 lp = lse_p[j * rows:(j + 1) * rows]
-                lo = ls[picked, :]
-                sn = jnp.sum(hq[layer, g, j].astype(F32) * k_new, axis=1, keepdims=True) * scale
-                top = jnp.maximum(jnp.maximum(lp, lo), sn)
+                lo = lm[here, :]
+                top = jnp.maximum(lp, lo)
                 wp = jnp.exp(lp - top)
-                wo_ = jnp.exp(lo - top)
-                wn = jnp.exp(sn - top)
-                mixed = wp * o_rc[layer, g, j].astype(F32) + wo_ * os[picked, :] + wn * v_new
+                ws = jnp.exp(lo - top)
+                mixed = wp * o_rc[layer, g, j].astype(F32) + ws * qs[here, :]
                 at = (par * group + j) * hd
-                o_cat[layer, core, tc, :, at:at + hd] = (mixed / (wp + wo_ + wn)).astype(BF16)
+                o_cat[layer, core, tc, :, at:at + hd] = (mixed / (wp + ws)).astype(BF16)
         send(o_cat.at[layer, core, tc], o_cat.at[layer, core, tc], oc_s.at[layer, t], oc_r.at[layer, t], partner)
 
     def project_out(layer, t):
@@ -270,9 +289,9 @@
         arrived(o_cat.at[layer, other, tc], oc_r.at[layer, t], oc_s.at[layer, t])
         lhs = jnp.concatenate([o_cat[layer, 0, tc], o_cat[layer, 1, tc]], axis=0)
 
-        @pl.loop(0, nblk)
-        def _(nb):
+        for nb in range(nblk):
             wo_copy(layer, tc, nb).wait()
+        for nb in range(nblk):
             upd = dot(lhs, wo_buf[tc, nb])
             if t == 0:
                 acc_o[nb] = upd
@@ -281,24 +300,36 @@
             if layer + 1 < layers:
                 wo_copy(layer + 1, tc, nb).start()
 
+    own = pl.ds(pl.multiple_of(core * rows, rows), rows)
+    theirs = pl.ds(pl.multiple_of(other * rows, rows), rows)
     for copy in prefix_copies(0):
         copy.start()
-    fetch_weights(0, 0, 4)
+    loads = [pltpu.make_async_copy(lens_hbm, lens, io_sem.at[0])]
+    for sd in range(2):
+        loads.append(pltpu.make_async_copy(hidden.at[:, sd * half:(sd + 1) * half], xh.at[0, sd, own, :], io_sem.at[1 + sd]))
+    for copy in loads:
+        copy.start()
+    fetch_weights(0, 0, RING)
     barrier = pltpu.get_barrier_semaphore()
     for d in range(1, ctx_size):
         pl.semaphore_signal(barrier, inc=1, device_id=to((me + d) % ctx_size), device_id_type=MESH)
+    relayout_prefix(0, 0)
+    for copy in loads:
+        copy.wait()
     pl.semaphore_wait(barrier, ctx_size - 1)
-    send(hidden, xr.at[core], xr_sem.at[0], xr_sem.at[1], partner)
-    fetch_weights(0, 4, RING)
-    xr[core] = hidden[...]
-    relayout_prefix(0)
-    send_prefix(0)
-    arrived(xr.at[other], xr_sem.at[1], xr_sem.at[0])
-    for sd in range(2):
-        for cr in range(2):
-            xh[0, sd, cr * rows:(cr + 1) * rows, :] = xr[cr, :, sd * half:(sd + 1) * half]
+    send(xh.at[0, :, own, :], xh.at[0, :, own, :], x_sem.at[2, 0], x_sem.at[2, 1], partner)
+    send_prefix(0, 0)
+    relayout_prefix(0, 1)
+    send_prefix(0, 1)
+    arrived(xh.at[0, :, theirs, :], x_sem.at[2, 1], x_sem.at[2, 0])
 
     for layer in range(layers):
+        if layer > 0:
+            for t in range(chips):
+                acc[t] = dots(layer, (2 * t, 2 * t + 1))
+                for n in (2 * t, 2 * t + 1):
+                    fetch_weights(layer, n + RING, n + RING + 1)
+            arrived(xh.at[layer, other], x_sem.at[0, 1], x_sem.at[0, 0])
         for t in range(chips):
             project(layer, t)
             if layer == 0 and t == 1:
@@ -311,13 +342,17 @@
             suffix_attention(layer)
             for copy in suffix_copies(layer + 1):
                 copy.start()
-            relayout_prefix(layer + 1)
-        await_prefix(layer)
-        for t in range(chips):
-            prefix_attention(layer, t)
-        if layer + 1 < layers:
-            send_prefix(layer + 1)
+            for kv in range(2):
+                relayout_prefix(layer + 1, kv)
+            await_prefix(layer)
+            for t in range(chips):
+                prefix_attention(layer, t)
+            for kv in range(2):
+                send_prefix(layer + 1, kv)
         else:
+            await_prefix(layer)
+            for t in (3, 0, 1, 2):
+                prefix_attention(layer, t)
             suffix_attention(layer)
         for t in range(chips):
             combine(layer, t)
@@ -334,22 +369,23 @@
                     fin_st[cr, :, cols] = new[cr * rows:(cr + 1) * rows]
         if layer + 1 < layers:
             send(xh.at[layer + 1, core], xh.at[layer + 1, core], x_sem.at[0, 0], x_sem.at[0, 1], partner)
-            arrived(xh.at[layer + 1, other], x_sem.at[0, 1], x_sem.at[0, 0])
     send(fin_st.at[other], fin_rc, x_sem.at[1, 0], x_sem.at[1, 1], partner)
-    hid_out[core] = fin_st[core]
-    for layer in range(layers):
-        for g in range(heads):
-            for i in range(2):
-                kvn_out[layer, g, i] = hq[layer, g, group + i]
+    stores = [pltpu.make_async_copy(fin_st.at[core], hid_out.at[core], io_sem.at[0]),
+              pltpu.make_async_copy(hq.at[:, :, group:group + 2], kvn_out, io_sem.at[1])]
+    for copy in stores:
+        copy.start()
     arrived(fin_rc, x_sem.at[1, 1], x_sem.at[1, 0])
-    hid_out[other] = fin_rc[...]
+    stores.append(pltpu.make_async_copy(fin_rc, hid_out.at[other], io_sem.at[2]))
+    stores[2].start()
+    for copy in stores:
+        copy.wait()
     for copy in pending:
         copy.wait_send()
 
 
-def cache_kernel(lens, hid, kvn, ksuf, vsuf, hid_out, kout, vout, buf, tiles, in_sem, out_sem):
+def cache_kernel(lens, hid, kvn, ksuf, vsuf, hid_out, kout, vout, buf, tiles, hbuf, kvbuf, in_sem, out_sem, io_sem):
     layers, batch = ksuf.shape[0], ksuf.shape[1]
-    heads, hd = ksuf.shape[3], ksuf.shape[4]
+    heads = ksuf.shape[3]
     half = hid.shape[2]
     step = 8
     parts = batch // step
@@ -363,21 +399,30 @@
         return pltpu.make_async_copy(srcs[i].at[layer, here], buf.at[layer, i, here], in_sem.at[at])
 
     todo = [(layer, i, part) for layer in range(layers) for i in range(2) for part in range(parts)]
+    news = pltpu.make_async_copy(kvn, kvbuf, io_sem.at[0])
+    news.start()
     for layer, i, part in todo:
         copies(layer, i, part, False).start()
-    for sd in range(2):
-        hid_out[:, sd * half:(sd + 1) * half] = hid[sd]
+    sides = [pltpu.make_async_copy(hid.at[sd], hbuf.at[:, sd * half:(sd + 1) * half], io_sem.at[1 + sd]) for sd in range(2)]
+    for copy in sides:
+        copy.start()
+    news.wait()
     for layer in range(layers):
         for i in range(2):
             for g in range(heads):
-                tiles[layer, i, pl.ds(g, batch, stride=heads), :] = kvn[layer, g, i].astype(F32)
+                tiles[layer, i, pl.ds(g, batch, stride=heads), :] = kvbuf[layer, g, i].astype(F32)
     for layer, i, part in todo:
         copies(layer, i, part, False).wait()
         for b in range(part * step, (part + 1) * step):
             buf[layer, i, b, lens[b]] = tiles[layer, i, b * heads:(b + 1) * heads, :].astype(BF16)
         copies(layer, i, part, True).start()
+    for copy in sides:
+        copy.wait()
+    whole = pltpu.make_async_copy(hbuf, hid_out, io_sem.at[3])
+    whole.start()
     for layer, i, part in todo:
         copies(layer, i, part, True).wait()
+    whole.wait()
 
 
 def solution(mesh):
@@ -401,19 +446,19 @@
         dma = pltpu.SemaphoreType.DMA
         spec = pl.BlockSpec
         scratch = [
-            vmem((RING, kc, group * hd), BF16), vmem((RING, kc, 2 * hd), BF16), dma((RING, 3)),
+            smem((rows,), jnp.int32), dma((3,)),
+            vmem((RING, kc, (group + 2) * hd), BF16), dma((RING, 3)),
             vmem((chips, nblk, 2 * group * hd, COLS), BF16), dma((chips, nblk)),
             vmem((2, span, heads, hd), BF16), dma((2,)), vmem((64 * heads, hd), F32),
             vmem((layers, ctx_size, 2, span, hd), BF16), vmem((layers, 2, ctx_size, span, hd), BF16),
-            dma((layers, ctx_size)), dma((layers, ctx_size)),
+            dma((layers, 2, ctx_size)), dma((layers, 2, ctx_size)),
             vmem((2, rows, slots * heads, hd), BF16), dma((2,)),
-            vmem((2, rows, dim), BF16), dma((2,)),
-            vmem((layers, 2, 2 * rows, half), BF16), vmem((2, rows, half), BF16), vmem((rows, half), BF16), dma((2, 2)),
-            vmem((2 * rows, group * hd), F32), vmem((2 * rows, 2 * hd), F32),
+            vmem((layers, 2, 2 * rows, half), BF16), vmem((2, rows, half), BF16), vmem((rows, half), BF16), dma((3, 2)),
+            vmem((chips, 2 * rows, (group + 2) * hd), F32),
             vmem((layers, chips, 2, group + 2, rows, hd), BF16), vmem((layers, heads, group + 2, rows, hd), BF16),
             dma((layers, chips)), dma((layers, chips)),
             vmem((layers, chips, 2, group, rows, hd), BF16), dma((layers, chips)), dma((layers, chips)),
-            vmem((rows * qh, hd), F32), vmem((rows * qh, hd), F32), vmem((rows * qh, hd), F32),
+            vmem((rows * qh, hd), F32), vmem((rows * qh, hd), F32), vmem((rows * qh, hd), F32), vmem((rows * qh, hd), F32),
             vmem((ctx_size, 2 * group * rows, span), F32), vmem((2 * group * rows, ctx_size * span), BF16),
             vmem((layers, chips, 2, group, rows, hd), BF16), vmem((layers, chips, 2, 8, 128), F32),
             vmem((layers, heads, group, rows, hd), BF16), vmem((layers, heads, 8, 128), F32),
@@ -426,8 +471,8 @@
             name="decode",
             out_shape=(jax.ShapeDtypeStruct((2, rows, half), BF16),
                        jax.ShapeDtypeStruct((layers, heads, 2, rows, hd), BF16)),
-            in_specs=[spec(memory_space=vmem), spec(memory_space=smem)] + [spec(memory_space=anym)] * 8,
-            out_specs=(spec(memory_space=vmem), spec(memory_space=vmem)),
+            in_specs=[spec(memory_space=anym)] * 10,
+            out_specs=(spec(memory_space=anym), spec(memory_space=anym)),
             scratch_shapes=scratch,
             compiler_params=pltpu.CompilerParams(collective_id=0, has_side_effects=True, vmem_limit_bytes=67043328),
         )(hidden, seq_lens, w_query, w_key, w_value, w_out, k_prefix, v_prefix,
@@ -438,11 +483,11 @@
             name="caches",
             out_shape=(jax.ShapeDtypeStruct(hidden.shape, BF16), jax.ShapeDtypeStruct(k_suffix.shape, BF16),
                        jax.ShapeDtypeStruct(v_suffix.shape, BF16)),
-            in_specs=[spec(memory_space=smem), spec(memory_space=vmem), spec(memory_space=vmem),
-                      spec(memory_space=anym), spec(memory_space=anym)],
-            out_specs=(spec(memory_space=vmem), spec(memory_space=anym), spec(memory_space=anym)),
+            in_specs=[spec(memory_space=smem)] + [spec(memory_space=anym)] * 4,
+            out_specs=(spec(memory_space=anym), spec(memory_space=anym), spec(memory_space=anym)),
             scratch_shapes=[vmem((layers, 2, rows, slots, heads, hd), BF16), vmem((layers, 2, rows * heads, hd), F32),
-                            dma((copies,)), dma((copies,))],
+                            vmem((rows, dim), BF16), vmem((layers, heads, 2, rows, hd), BF16),
+                            dma((copies,)), dma((copies,)), dma((4,))],
             compiler_params=pltpu.CompilerParams(vmem_limit_bytes=67043328),
         )(seq_lens, hid, kvn, k_suffix, v_suffix)
 

time: 91.8 us -> 84.7 us (0.923)
  Pallas kernels: 90.9 us -> 83.8 us
    pallas_call x1, Pallas kernels: 82.5 us -> 76.3 us  [local_step(): pl.pallas_call(functools.partial(decode_kernel, ctx_size), name='decode',...]
where the time goes in v1:
time: 84.7 us; the launch traced here: 84.6 us
  Pallas kernels  83.8 us (99%)
    pallas_call x1, Pallas kernels, local_step(): pl.pallas_call(functools.partial(decode_kernel, ctx_size), name='decode',...  76.3 us
    pallas_call x1, Pallas kernels, local_step(): pl.pallas_call(cache_kernel, name='caches', out_shape=(jax.ShapeDtypeStru...  7.42 us

profile of v1, /device:TPU:81, one launch (start us, length us, event | category | flops | bytes accessed | tf_op | source)
XLA Modules:
  0.0 84.6 jit_solution(11441179652222816413)
XLA Ops:
  0.6 76.3 %decode.1 = (bf16[2,32,2560]{2,1,0:T(8,128)(2,1)}, bf16[2,8,2,32,128]{4,3,2,1,0:T(8,128)(2,1)}) custom-call(bf16[32,5120]{1,0:T(8,128)(2,1)} %hidden.1, s32[32]{0:T(128)} %lens.1, bf16[2,5120,4096]{2,1,0:T(8,128)(2,1)} %wq.1, bf16[2,5120,1024]{2,1,0:T(8,128)(2,1)} %wk.1, bf16[2,5120,1024]{2,1,0:T(8,128)(2,1)} %wv.1, bf16[2,4096,5120]{2,1,0:T(8,128)(2,1)} %wo.1, ...), custom_call_target="tpu_custom_call" | custom-call | tf_op jit(solution)/shard_map/decode/pallas_call | solution.py:469
  77.0 7.4 %caches.1 = (bf16[32,5120]{1,0:T(8,128)(2,1)}, bf16[2,32,32,8,128]{4,3,2,1,0:T(8,128)(2,1)}, bf16[2,32,32,8,128]{4,3,2,1,0:T(8,128)(2,1)}) custom-call(s32[32]{0:T(128)} %lens.1, bf16[2,32,2560]{2,1,0:T(8,128)(2,1)} %get-tuple-element.5.hid, bf16[2,8,2,32,128]{4,3,2,1,0:T(8,128)(2,1)} %get-tuple-element.6.kvn, bf16[2,32,32,8,128]{4,3,2,1,0:T(8,128)(2,1)} %ksuf.1, ...), custom_call_target="tpu_custom_call" | custom-call | tf_op jit(solution)/shard_map/caches/pallas_call | solution.py:481

commit v2 on v1

--- a/solution.py
+++ b/solution.py
@@ -12,6 +12,7 @@
 F32 = jnp.float32
 RING = 10
 COLS = 512
+PAD = 8
 LOG2E = 1.4426950408889634
 FLOOR = float(jnp.finfo(jnp.float32).min)
 
@@ -44,6 +45,7 @@
     c2 = scale * LOG2E
     gq = group * hd
     nblk = half // COLS
+    pitch = qh + PAD
 
     me = lax.axis_index("ctx")
     chip = me // 2
@@ -179,24 +181,26 @@
         send(qkv_st.at[layer, t, other], hq.at[layer, g], hs_s.at[layer, t], hs_r.at[layer, t], partner)
         hq[layer, g] = qkv_st[layer, t, core]
 
-    def suffix_attention(layer):
+    def suffix_queries(layer):
         for t in range(chips):
             arrived(hq.at[layer, dest_chip(t) * 2 + other], hs_r.at[layer, t], hs_s.at[layer, t])
         for g in range(heads):
             for j in range(group):
-                qs[pl.ds(g * group + j, rows, stride=heads * group), :] = hq[layer, g, j].astype(F32)
+                qs[pl.ds(g * group + j, rows, stride=pitch), :] = hq[layer, g, j].astype(F32)
         for copy in suffix_copies(layer):
             copy.wait()
+
+    def suffix_attention(layer, first, last):
         row_id = lax.broadcasted_iota(jnp.int32, (qh, slots * heads), 0)
         col_id = lax.broadcasted_iota(jnp.int32, (qh, slots * heads), 1)
         slot_of = jnp.where((row_id // group) == (col_id % heads), col_id // heads, slots)
         step = 8
 
-        @pl.loop(0, rows // step)
+        @pl.loop(first // step, last // step)
         def _(blk):
             for i in range(step):
                 b = blk * step + i
-                base = pl.multiple_of(b * qh, qh)
+                base = pl.multiple_of(b * pitch, 8)
                 s = dot_t(qs[pl.ds(base, qh), :].astype(BF16), suf[0, b])
                 s = jnp.where(slot_of < lens[b], s, FLOOR)
                 m = jnp.max(s, axis=1, keepdims=True)
@@ -206,12 +210,13 @@
                 os[pl.ds(base, qh), :] = val * (1.0 / mass)
                 ls[pl.ds(base, qh), :] = jnp.broadcast_to(m * scale + jnp.log(mass), (qh, hd))
 
+    def suffix_merge(layer):
         for g in range(heads):
             k_new = hq[layer, g, group].astype(F32)
             v_new = hq[layer, g, group + 1].astype(F32)
             for j in range(group):
                 h = g * group + j
-                picked = pl.ds(h, rows, stride=qh)
+                picked = pl.ds(h, rows, stride=pitch)
                 lo = ls[picked, :]
                 sn = jnp.sum(hq[layer, g, j].astype(F32) * k_new, axis=1, keepdims=True) * scale
                 top = jnp.maximum(lo, sn)
@@ -333,27 +338,31 @@
         for t in range(chips):
             project(layer, t)
             if layer == 0 and t == 1:
-                for copy in suffix_copies(0):
+                for copy in suffix_copies(0) + prefix_copies(1):
                     copy.start()
         if layer + 1 < layers:
-            for copy in prefix_copies(layer + 1):
-                copy.start()
             fetch_weights(layer + 1, 0, RING)
-            suffix_attention(layer)
+            relayout_prefix(layer + 1, 0)
+            send_prefix(layer + 1, 0)
+            suffix_queries(layer)
+            suffix_attention(layer, 0, rows)
+            suffix_merge(layer)
             for copy in suffix_copies(layer + 1):
                 copy.start()
-            for kv in range(2):
-                relayout_prefix(layer + 1, kv)
+            relayout_prefix(layer + 1, 1)
             await_prefix(layer)
             for t in range(chips):
                 prefix_attention(layer, t)
-            for kv in range(2):
-                send_prefix(layer + 1, kv)
+            send_prefix(layer + 1, 1)
         else:
             await_prefix(layer)
-            for t in (3, 0, 1, 2):
+            prefix_attention(layer, chips - 1)
+            suffix_queries(layer)
+            suffix_attention(layer, 0, rows // 2)
+            for t in range(chips - 1):
                 prefix_attention(layer, t)
-            suffix_attention(layer)
+            suffix_attention(layer, rows // 2, rows)
+            suffix_merge(layer)
         for t in range(chips):
             combine(layer, t)
             if t > 0:
@@ -458,7 +467,8 @@
             vmem((layers, chips, 2, group + 2, rows, hd), BF16), vmem((layers, heads, group + 2, rows, hd), BF16),
             dma((layers, chips)), dma((layers, chips)),
             vmem((layers, chips, 2, group, rows, hd), BF16), dma((layers, chips)), dma((layers, chips)),
-            vmem((rows * qh, hd), F32), vmem((rows * qh, hd), F32), vmem((rows * qh, hd), F32), vmem((rows * qh, hd), F32),
+            vmem((rows * (qh + PAD), hd), F32), vmem((rows * (qh + PAD), hd), F32), vmem((rows * (qh + PAD), hd), F32),
+            vmem((rows * qh, hd), F32),
             vmem((ctx_size, 2 * group * rows, span), F32), vmem((2 * group * rows, ctx_size * span), BF16),
             vmem((layers, chips, 2, group, rows, hd), BF16), vmem((layers, chips, 2, 8, 128), F32),
             vmem((layers, heads, group, rows, hd), BF16), vmem((layers, heads, 8, 128), F32),

time: 84.7 us -> 82.1 us (0.969)
  Pallas kernels: 83.8 us -> 81.2 us
    pallas_call x1, Pallas kernels: 76.3 us -> 73.8 us  [local_step(): pl.pallas_call(functools.partial(decode_kernel, ctx_size), name='decode',...]
where the time goes in v2:
time: 82.1 us
  Pallas kernels  81.2 us (99%)
    pallas_call x1, Pallas kernels, local_step(): pl.pallas_call(functools.partial(decode_kernel, ctx_size), name='decode',...  73.8 us
    pallas_call x1, Pallas kernels, local_step(): pl.pallas_call(cache_kernel, name='caches', out_shape=(jax.ShapeDtypeStru...  7.42 us

profile of v2, /device:TPU:81, one launch (start us, length us, event | category | flops | bytes accessed | tf_op | source)
XLA Modules:
  0.0 82.1 jit_solution(2334905728204529006)
XLA Ops:
  0.6 73.8 %decode.1 = (bf16[2,32,2560]{2,1,0:T(8,128)(2,1)}, bf16[2,8,2,32,128]{4,3,2,1,0:T(8,128)(2,1)}) custom-call(bf16[32,5120]{1,0:T(8,128)(2,1)} %hidden.1, s32[32]{0:T(128)} %lens.1, bf16[2,5120,4096]{2,1,0:T(8,128)(2,1)} %wq.1, bf16[2,5120,1024]{2,1,0:T(8,128)(2,1)} %wk.1, bf16[2,5120,1024]{2,1,0:T(8,128)(2,1)} %wv.1, bf16[2,4096,5120]{2,1,0:T(8,128)(2,1)} %wo.1, ...), custom_call_target="tpu_custom_call" | custom-call | tf_op jit(solution)/shard_map/decode/pallas_call | solution.py:479
  74.5 7.4 %caches.1 = (bf16[32,5120]{1,0:T(8,128)(2,1)}, bf16[2,32,32,8,128]{4,3,2,1,0:T(8,128)(2,1)}, bf16[2,32,32,8,128]{4,3,2,1,0:T(8,128)(2,1)}) custom-call(s32[32]{0:T(128)} %lens.1, bf16[2,32,2560]{2,1,0:T(8,128)(2,1)} %get-tuple-element.5.hid, bf16[2,8,2,32,128]{4,3,2,1,0:T(8,128)(2,1)} %get-tuple-element.6.kvn, bf16[2,32,32,8,128]{4,3,2,1,0:T(8,128)(2,1)} %ksuf.1, ...), custom_call_target="tpu_custom_call" | custom-call | tf_op jit(solution)/shard_map/caches/pallas_call | solution.py:491

commit v3 on v2

--- a/solution.py
+++ b/solution.py
@@ -127,11 +127,14 @@
             for g in range(heads):
                 psend[layer, g, kv, pl.ds(base, step), :] = pf32[pl.ds(g, step, stride=heads), :].astype(BF16)
 
-    def send_prefix(layer, kv):
-        for d in (4, 5, 3, 2, 6, 7, 1):
-            dev = (me + d) % ctx_size
+    def send_prefix(layer, kv, far, near):
+        steps = ((2, core), (2, other), (0, other)) if far else ()
+        steps += ((1, core), (3, core), (1, other), (3, other)) if near else ()
+        for dc, cr in steps:
+            dev = ((chip + dc) % chips) * 2 + cr
             send(psend.at[layer, dev, kv], precv.at[layer, kv, me], ps_s.at[layer, kv, dev], ps_r.at[layer, kv, me], dev)
-        precv[layer, kv, me] = psend[layer, me, kv]
+        if near:
+            precv[layer, kv, me] = psend[layer, me, kv]
 
     def await_prefix(layer):
         for d in (1, 7, 2, 6, 3, 5, 4):
@@ -307,6 +310,9 @@
 
     own = pl.ds(pl.multiple_of(core * rows, rows), rows)
     theirs = pl.ds(pl.multiple_of(other * rows, rows), rows)
+    barrier = pltpu.get_barrier_semaphore()
+    for d in range(1, ctx_size):
+        pl.semaphore_signal(barrier, inc=1, device_id=to((me + d) % ctx_size), device_id_type=MESH)
     for copy in prefix_copies(0):
         copy.start()
     loads = [pltpu.make_async_copy(lens_hbm, lens, io_sem.at[0])]
@@ -314,18 +320,16 @@
         loads.append(pltpu.make_async_copy(hidden.at[:, sd * half:(sd + 1) * half], xh.at[0, sd, own, :], io_sem.at[1 + sd]))
     for copy in loads:
         copy.start()
-    fetch_weights(0, 0, RING)
-    barrier = pltpu.get_barrier_semaphore()
-    for d in range(1, ctx_size):
-        pl.semaphore_signal(barrier, inc=1, device_id=to((me + d) % ctx_size), device_id_type=MESH)
-    relayout_prefix(0, 0)
     for copy in loads:
         copy.wait()
+    fetch_weights(0, 0, 2)
+    relayout_prefix(0, 0)
     pl.semaphore_wait(barrier, ctx_size - 1)
     send(xh.at[0, :, own, :], xh.at[0, :, own, :], x_sem.at[2, 0], x_sem.at[2, 1], partner)
-    send_prefix(0, 0)
+    send_prefix(0, 0, True, True)
     relayout_prefix(0, 1)
-    send_prefix(0, 1)
+    send_prefix(0, 1, True, True)
+    fetch_weights(0, 2, RING)
     arrived(xh.at[0, :, theirs, :], x_sem.at[2, 1], x_sem.at[2, 0])
 
     for layer in range(layers):
@@ -343,7 +347,7 @@
         if layer + 1 < layers:
             fetch_weights(layer + 1, 0, RING)
             relayout_prefix(layer + 1, 0)
-            send_prefix(layer + 1, 0)
+            send_prefix(layer + 1, 0, True, False)
             suffix_queries(layer)
             suffix_attention(layer, 0, rows)
             suffix_merge(layer)
@@ -353,7 +357,8 @@
             await_prefix(layer)
             for t in range(chips):
                 prefix_attention(layer, t)
-            send_prefix(layer + 1, 1)
+            send_prefix(layer + 1, 0, False, True)
+            send_prefix(layer + 1, 1, True, True)
         else:
             await_prefix(layer)
             prefix_attention(layer, chips - 1)
@@ -392,7 +397,7 @@
         copy.wait_send()
 
 
-def cache_kernel(lens, hid, kvn, ksuf, vsuf, hid_out, kout, vout, buf, tiles, hbuf, kvbuf, in_sem, out_sem, io_sem):
+def cache_kernel(lens_hbm, hid, kvn, ksuf, vsuf, hid_out, kout, vout, lens, buf, tiles, hbuf, kvbuf, in_sem, out_sem, io_sem):
     layers, batch = ksuf.shape[0], ksuf.shape[1]
     heads = ksuf.shape[3]
     half = hid.shape[2]
@@ -410,12 +415,15 @@
     todo = [(layer, i, part) for layer in range(layers) for i in range(2) for part in range(parts)]
     news = pltpu.make_async_copy(kvn, kvbuf, io_sem.at[0])
     news.start()
+    lengths = pltpu.make_async_copy(lens_hbm, lens, io_sem.at[4])
+    lengths.start()
     for layer, i, part in todo:
         copies(layer, i, part, False).start()
     sides = [pltpu.make_async_copy(hid.at[sd], hbuf.at[:, sd * half:(sd + 1) * half], io_sem.at[1 + sd]) for sd in range(2)]
     for copy in sides:
         copy.start()
     news.wait()
+    lengths.wait()
     for layer in range(layers):
         for i in range(2):
             for g in range(heads):
@@ -493,11 +501,12 @@
             name="caches",
             out_shape=(jax.ShapeDtypeStruct(hidden.shape, BF16), jax.ShapeDtypeStruct(k_suffix.shape, BF16),
                        jax.ShapeDtypeStruct(v_suffix.shape, BF16)),
-            in_specs=[spec(memory_space=smem)] + [spec(memory_space=anym)] * 4,
+            in_specs=[spec(memory_space=anym)] * 5,
             out_specs=(spec(memory_space=anym), spec(memory_space=anym), spec(memory_space=anym)),
-            scratch_shapes=[vmem((layers, 2, rows, slots, heads, hd), BF16), vmem((layers, 2, rows * heads, hd), F32),
+            scratch_shapes=[smem((rows,), jnp.int32), vmem((layers, 2, rows, slots, heads, hd), BF16),
+                            vmem((layers, 2, rows * heads, hd), F32),
                             vmem((rows, dim), BF16), vmem((layers, heads, 2, rows, hd), BF16),
-                            dma((copies,)), dma((copies,)), dma((4,))],
+                            dma((copies,)), dma((copies,)), dma((5,))],
             compiler_params=pltpu.CompilerParams(vmem_limit_bytes=67043328),
         )(seq_lens, hid, kvn, k_suffix, v_suffix)
 

time: 82.1 us -> 75.5 us (0.920)
  Pallas kernels: 81.2 us -> 74.6 us
    pallas_call x1, Pallas kernels: 73.8 us -> 68 us  [local_step(): pl.pallas_call(functools.partial(decode_kernel, ctx_size), name='decode',...]
where the time goes in v3:
time: 75.5 us; the launch traced here: 75.4 us
  Pallas kernels  74.6 us (99%)
  between operations  0.82 us (1%)
    pallas_call x1, Pallas kernels, local_step(): pl.pallas_call(functools.partial(decode_kernel, ctx_size), name='decode',...  68 us
    pallas_call x1, Pallas kernels, local_step(): pl.pallas_call(cache_kernel, name='caches', out_shape=(jax.ShapeDtypeStru...  6.62 us

profile of v3, /device:TPU:81, one launch (start us, length us, event | category | flops | bytes accessed | tf_op | source)
XLA Modules:
  0.0 75.4 jit_solution(4002744092907697532)
XLA Ops:
  0.6 68.0 %decode.1 = (bf16[2,32,2560]{2,1,0:T(8,128)(2,1)}, bf16[2,8,2,32,128]{4,3,2,1,0:T(8,128)(2,1)}) custom-call(bf16[32,5120]{1,0:T(8,128)(2,1)} %hidden.1, s32[32]{0:T(128)} %lens_hbm.3, bf16[2,5120,4096]{2,1,0:T(8,128)(2,1)} %wq.1, bf16[2,5120,1024]{2,1,0:T(8,128)(2,1)} %wk.1, bf16[2,5120,1024]{2,1,0:T(8,128)(2,1)} %wv.1, bf16[2,4096,5120]{2,1,0:T(8,128)(2,1)} %wo.1, ...), custom_call_target="tpu_custom_call" | custom-call | tf_op jit(solution)/shard_map/decode/pallas_call | solution.py:487
  68.6 6.6 %caches.1 = (bf16[32,5120]{1,0:T(8,128)(2,1)}, bf16[2,32,32,8,128]{4,3,2,1,0:T(8,128)(2,1)}, bf16[2,32,32,8,128]{4,3,2,1,0:T(8,128)(2,1)}) custom-call(s32[32]{0:T(128)} %lens_hbm.3, bf16[2,32,2560]{2,1,0:T(8,128)(2,1)} %get-tuple-element.5.hid, bf16[2,8,2,32,128]{4,3,2,1,0:T(8,128)(2,1)} %get-tuple-element.6.kvn, bf16[2,32,32,8,128]{4,3,2,1,0:T(8,128)(2,1)} %ksuf.1, ...), custom_call_target="tpu_custom_call" | custom-call | tf_op jit(solution)/shard_map/caches/pallas_call | solution.py:499

commit v4 on v3

--- a/solution.py
+++ b/solution.py
@@ -136,11 +136,10 @@
         if near:
             precv[layer, kv, me] = psend[layer, me, kv]
 
-    def await_prefix(layer):
+    def await_prefix(layer, kv):
         for d in (1, 7, 2, 6, 3, 5, 4):
             src = (me + d) % ctx_size
-            for kv in range(2):
-                arrived(precv.at[layer, kv, src], ps_r.at[layer, kv, src], ps_s.at[layer, kv, src])
+            arrived(precv.at[layer, kv, src], ps_r.at[layer, kv, src], ps_s.at[layer, kv, src])
 
     def dots(layer, chunks):
         for n in chunks:
@@ -164,9 +163,9 @@
         qkv = total.astype(BF16)
         for n in chunks:
             fetch_weights(layer, n + RING, n + RING + 1)
-        if layer == 0 and t >= 2:
-            fetch_wo(0, 2 * (t - 2))
-            fetch_wo(0, 2 * (t - 2) + 1)
+        if t >= 2:
+            fetch_wo(layer, 2 * (t - 2))
+            fetch_wo(layer, 2 * (t - 2) + 1)
 
         for cr in range(2):
             part = slice(cr * rows, (cr + 1) * rows)
@@ -249,6 +248,8 @@
                 mass = mass + e[:, lo:lo + 128]
             pb[:, s * span:(s + 1) * span] = e.astype(BF16)
         mass = jnp.sum(mass, axis=1, keepdims=True)
+        if t == (0 if layer == 0 else chips - 1):
+            await_prefix(layer, 1)
         vals = dot(pb[...], precv[layer, 1].reshape(ctx_size * span, hd))
         out = (vals * (1.0 / mass)).astype(BF16)
         lse = jnp.broadcast_to(m * scale + jnp.log(mass), (2 * group * rows, 128)).T
@@ -305,8 +306,6 @@
                 acc_o[nb] = upd
             else:
                 acc_o[nb] += upd
-            if layer + 1 < layers:
-                wo_copy(layer + 1, tc, nb).start()
 
     own = pl.ds(pl.multiple_of(core * rows, rows), rows)
     theirs = pl.ds(pl.multiple_of(other * rows, rows), rows)
@@ -354,13 +353,13 @@
             for copy in suffix_copies(layer + 1):
                 copy.start()
             relayout_prefix(layer + 1, 1)
-            await_prefix(layer)
+            await_prefix(layer, 0)
             for t in range(chips):
                 prefix_attention(layer, t)
             send_prefix(layer + 1, 0, False, True)
             send_prefix(layer + 1, 1, True, True)
         else:
-            await_prefix(layer)
+            await_prefix(layer, 0)
             prefix_attention(layer, chips - 1)
             suffix_queries(layer)
             suffix_attention(layer, 0, rows // 2)
@@ -417,7 +416,8 @@
     news.start()
     lengths = pltpu.make_async_copy(lens_hbm, lens, io_sem.at[4])
     lengths.start()
-    for layer, i, part in todo:
+    ahead = len(todo) // 2
+    for layer, i, part in todo[:ahead]:
         copies(layer, i, part, False).start()
     sides = [pltpu.make_async_copy(hid.at[sd], hbuf.at[:, sd * half:(sd + 1) * half], io_sem.at[1 + sd]) for sd in range(2)]
     for copy in sides:
@@ -428,8 +428,10 @@
         for i in range(2):
             for g in range(heads):
                 tiles[layer, i, pl.ds(g, batch, stride=heads), :] = kvbuf[layer, g, i].astype(F32)
-    for layer, i, part in todo:
+    for n, (layer, i, part) in enumerate(todo):
         copies(layer, i, part, False).wait()
+        for ahead_of in todo[n + ahead:n + ahead + 1]:
+            copies(*ahead_of, False).start()
         for b in range(part * step, (part + 1) * step):
             buf[layer, i, b, lens[b]] = tiles[layer, i, b * heads:(b + 1) * heads, :].astype(BF16)
         copies(layer, i, part, True).start()

time: 75.5 us -> 75.8 us (level)
  no operation moved by 1% of the time
where the time goes in v4:
time: 75.8 us; the launch traced here: 75.7 us
  Pallas kernels  74.8 us (99%)
  between operations  0.82 us (1%)
    pallas_call x1, Pallas kernels, local_step(): pl.pallas_call(functools.partial(decode_kernel, ctx_size), name='decode',...  67.6 us
    pallas_call x1, Pallas kernels, local_step(): pl.pallas_call(cache_kernel, name='caches', out_shape=(jax.ShapeDtypeStru...  7.28 us

profile of v4, /device:TPU:81, one launch (start us, length us, event | category | flops | bytes accessed | tf_op | source)
XLA Modules:
  0.0 75.7 jit_solution(14167453286907090686)
XLA Ops:
  0.6 67.6 %decode.1 = (bf16[2,32,2560]{2,1,0:T(8,128)(2,1)}, bf16[2,8,2,32,128]{4,3,2,1,0:T(8,128)(2,1)}) custom-call(bf16[32,5120]{1,0:T(8,128)(2,1)} %hidden.1, s32[32]{0:T(128)} %lens_hbm.3, bf16[2,5120,4096]{2,1,0:T(8,128)(2,1)} %wq.1, bf16[2,5120,1024]{2,1,0:T(8,128)(2,1)} %wk.1, bf16[2,5120,1024]{2,1,0:T(8,128)(2,1)} %wv.1, bf16[2,4096,5120]{2,1,0:T(8,128)(2,1)} %wo.1, ...), custom_call_target="tpu_custom_call" | custom-call | tf_op jit(solution)/shard_map/decode/pallas_call | solution.py:489
  68.2 7.3 %caches.1 = (bf16[32,5120]{1,0:T(8,128)(2,1)}, bf16[2,32,32,8,128]{4,3,2,1,0:T(8,128)(2,1)}, bf16[2,32,32,8,128]{4,3,2,1,0:T(8,128)(2,1)}) custom-call(s32[32]{0:T(128)} %lens_hbm.3, bf16[2,32,2560]{2,1,0:T(8,128)(2,1)} %get-tuple-element.5.hid, bf16[2,8,2,32,128]{4,3,2,1,0:T(8,128)(2,1)} %get-tuple-element.6.kvn, bf16[2,32,32,8,128]{4,3,2,1,0:T(8,128)(2,1)} %ksuf.1, ...), custom_call_target="tpu_custom_call" | custom-call | tf_op jit(solution)/shard_map/caches/pallas_call | solution.py:501
